TPU v7x, 64 devices: a 2x2x8 block of a 4x4x8 slice. The times are simulated.
64 devices in a mesh: dp: 4 (over x, y), pp: 16 (over z, core).
Axes of the slice: x: 2, y: 2, z: 8, core: 2. Of those that a mesh axis runs over, the one named last changes fastest.
The devices are a block of a 4x4x8 slice.
Arguments:
- x_final: bfloat16 [8192, 768], P(('dp', 'pp')), parts along dimension 0
- w_vocab: bfloat16 [50304, 768], P('pp')
- labels: int32 [8192], P('dp'), parts along dimension 0
- tok_mask: int32 [8192], P('dp'), parts along dimension 0
- next_ids: int32 [8192], P('dp'), parts along dimension 0
- d_embed: bfloat16 [8192, 768], P(('dp', 'pp')), parts along dimension 0
- act_in: bfloat16 [64, 2048, 768], P(('dp', 'pp')), parts along dimension 0
- w_up: bfloat16 [16, 768, 3072], P('pp')
- w_down: bfloat16 [16, 3072, 768], P('pp')
Outputs:
- output 1: float32 [4], P('dp'), parts along dimension 0
- output 2: float32 [8192, 768], P(('dp', 'pp')), parts along dimension 0
- output 3: bfloat16 [201216, 768], P(('dp', 'pp')), parts along dimension 0
- output 4: bfloat16 [8192, 768], P(('dp', 'pp')), parts along dimension 0
- output 5: bfloat16 [64, 2048, 768], P(('dp', 'pp')), parts along dimension 0
There are 4 independent parts. A program takes and returns all parts, laid end to end along the dimension named above; an argument that names none is the same for every part.
All inputs are finite; a program needn't handle non-finite values.
Results may differ from a plain program's by a relative error of at most 0.001.
Values are sent between devices in bfloat16 or wider.
A program may use at most 768 MiB of HBM per device.

v0:
```python
import math
import jax
import jax.numpy as jnp
from jax import lax
from jax.sharding import PartitionSpec as P


def solution(mesh):
    def local_step(x_rows, w_slice, labels, tok_mask, next_ids, d_rows, act_in, w_up, w_down):
        vocab_rows, model_dim = w_slice.shape
        emb_scale = math.sqrt(model_dim)
        offset = lax.axis_index("pp") * vocab_rows
        x_full = lax.all_gather(x_rows, "pp", axis=0, tiled=True)
        d_full = lax.all_gather(d_rows, "pp", axis=0, tiled=True)
        logits = jnp.einsum("td,vd->tv", x_full, w_slice, preferred_element_type=jnp.float32)
        local_ids = lax.broadcasted_iota(jnp.int32, (1, vocab_rows), 1)
        label_hit = local_ids == (labels - offset)[:, None]
        row_max = lax.pmax(jnp.max(logits, axis=1), "pp")
        exp_logits = jnp.exp(logits - row_max[:, None])
        row_stats = lax.psum(jnp.stack([jnp.sum(exp_logits, axis=1), jnp.sum(jnp.where(label_hit, logits, 0.0), axis=1)]), "pp")
        row_total = row_stats[0]
        target = row_stats[1]
        weight = tok_mask.astype(jnp.float32)
        kept_count = jnp.maximum(jnp.sum(weight), 1.0)
        mean_loss = jnp.sum(weight * (jnp.log(row_total) + row_max - target)) / kept_count
        grad_logits = ((exp_logits / row_total[:, None] - label_hit.astype(jnp.float32)) * (weight / kept_count)[:, None]).astype(jnp.bfloat16)
        d_part = jnp.dot(grad_logits, w_slice, preferred_element_type=jnp.float32)
        d_hidden = lax.psum_scatter(d_part, "pp", scatter_dimension=0, tiled=True)
        d_head = jnp.einsum("tv,td->vd", grad_logits, x_full, preferred_element_type=jnp.float32)
        id_hit = (local_ids == (next_ids - offset)[:, None]).astype(jnp.bfloat16)
        d_table = jnp.einsum("tv,td->vd", id_hit, d_full, preferred_element_type=jnp.float32)
        d_vocab = (d_head + d_table * emb_scale).astype(jnp.bfloat16)
        local_pos = next_ids - offset
        in_share = (local_pos >= 0) & (local_pos < vocab_rows)
        picked_rows = w_slice[jnp.clip(local_pos, 0, vocab_rows - 1)]
        embed_part = jnp.where(in_share[:, None], picked_rows.astype(jnp.float32) * emb_scale, 0.0).astype(jnp.bfloat16)
        embed_out = lax.psum_scatter(embed_part, "pp", scatter_dimension=0, tiled=True)
        hidden = jax.nn.gelu(jnp.dot(act_in[0], w_up[0], preferred_element_type=jnp.float32)).astype(jnp.bfloat16)
        mlp_out = (act_in[0].astype(jnp.float32) + jnp.dot(hidden, w_down[0], preferred_element_type=jnp.float32)).astype(jnp.bfloat16)
        return mean_loss.reshape(1), d_hidden, d_vocab, embed_out, mlp_out[None]

    token_spec = P(("dp", "pp"))
    return jax.shard_map(
        local_step,
        mesh=mesh,
        in_specs=(token_spec, P("pp"), P("dp"), P("dp"), P("dp"), token_spec, token_spec, P("pp"), P("pp")),
        out_specs=(P("dp"), token_spec, token_spec, token_spec, token_spec),
        check_vma=False,
    )
```

profile of v0, /device:TPU:21, one launch (start us, length us, event | category | flops | bytes accessed | tf_op | source)
XLA Modules:
  0.0 254.5 jit_solution(561193667600106531)
XLA Ops:
  7.2 0.1 all-gather.3.cloned.1.call-start
  7.2 0.7 all-gather.3.cloned.1.call-update
  8.0 0.1 all-gather.5.cloned.1.call-start
  8.0 0.7 all-gather.5.cloned.1.call-update
  8.8 0.1 reduce-scatter.5.cloned.1.call-start
  8.9 0.7 compare_and_fusion
  9.6 11.5 %gather_fusion = bf16[2048,768]{1,0:T(8,128)(2,1)S(1)} fusion(bf16[3144,768]{1,0:T(8,128)(2,1)} %param.10, s32[2048]{0:T(1024)S(1)} %fusion.35), kind=kCustom, calls=%fused_computation | custom fusion | bytes 6299648 | tf_op jit(solution)/shard_map/gather | solution.py:35
  21.0 0.0 copy-start.2
  21.0 2.1 select_convert_fusion
  23.2 0.1 reduce-scatter.5.cloned.1.call-update
  23.2 0.1 reduce-scatter.3.cloned.1.call-start
  23.3 0.0 copy-done.2
  23.3 28.9 %all-gather.3.cloned.1.call-done = bf16[2048,768]{1,0:T(8,128)(2,1)} async-done(((bf16[128,768]{1,0:T(8,128)(2,1)}), bf16[2048,768]{1,0:T(8,128)(2,1)}) %all-gather.3.cloned.1.call-update) | async-done | bytes 3145744 | tf_op jit(solution)/shard_map/all_gather | solution.py:13
  52.2 17.9 %fusion.41 = (f32[2048]{0:T(1024)S(1)}, f32[2048,3144]{0,1:T(8,128)}) fusion(bf16[2048,768]{1,0:T(8,128)(2,1)} %all-gather.3.cloned.1.call-done, bf16[3144,768]{1,0:T(8,128)(2,1)} %param.10), kind=kOutput, calls=%fused_computation.41 | convolution fusion | flops 9896605696 | bytes 33738752 | tf_op jit(solution)/shard_map/td,vd->tv/dot_general | solution.py:15
  70.1 24.4 %pmax.7 = f32[2048]{0:T(1024)S(1)} all-reduce(f32[2048]{0:T(1024)S(1)} %get-tuple-element.13), channel_id=1, replica_groups=mesh['dp'=4,'pp'=16] {'pp'}, use_global_device_ids=true, to_apply=%region_1.0 | all-reduce | flops 2048 | bytes 16384 | tf_op jit(solution)/shard_map/pmax | solution.py:18
  94.6 0.0 copy-start.1
  94.6 0.0 slice-start
  94.6 11.9 %fusion.9 = (f32[2048]{0:T(1024)S(1)}, f32[2048]{0:T(1024)S(1)}) fusion(f32[2048,3144]{0,1:T(8,128)} %get-tuple-element.14, f32[2048]{0:T(1024)S(1)} %pmax.7, s32[2048]{0:T(1024)S(1)} %broadcast_subtract_fusion.1), kind=kLoop, calls=%fused_computation.16 | loop fusion | flops 32190464 | bytes 25788416 | tf_op jit(solution)/shard_map/reduce_sum | solution.py:20
  106.5 44.7 %psum.7 = f32[2,2048]{1,0:T(2,128)S(1)} all-reduce(f32[2,2048]{1,0:T(2,128)S(1)} %pad_maximum_fusion), channel_id=1, replica_groups=mesh['dp'=4,'pp'=16] {'pp'}, use_global_device_ids=true, to_apply=%region_4.5 | all-reduce | flops 4096 | bytes 32768 | tf_op jit(solution)/shard_map/psum | solution.py:20
  151.3 0.0 copy-done.1
  151.3 0.6 convert_reduce_fusion
  152.6 0.0 slice-start.1
  152.6 12.6 %multiply_convert_fusion = bf16[2048,3144]{0,1:T(8,128)(2,1)S(1)} fusion(f32[2048,3144]{0,1:T(8,128)} %get-tuple-element.14, f32[2048]{0:T(1024)S(1)} %convert_divide_fusion, f32[2048]{0:T(1024)S(1)} %bitcast.38, s32[2048]{0:T(1024)S(1)} %broadcast_subtract_fusion.1, f32[2048]{0:T(1024)S(1)} %pmax.7), kind=kLoop, calls=%fused_computation.4 | loop fusion | flops 45072384 | bytes 38666240 | tf_op jit(solution)/shard_map/convert_element_type | solution.py:26
  165.2 4.6 %copy-done = bf16[2048,3144]{0,1:T(8,128)(2,1)} copy-done((bf16[2048,3144]{0,1:T(8,128)(2,1)}, bf16[2048,3144]{0,1:T(8,128)(2,1)S(1)}, u32[]{:S(2)}) %copy-start) | copy-done | bytes 12877848
  169.8 0.0 slice-done
  169.8 13.4 %fusion.42 = f32[2048,768]{1,0:T(8,128)} fusion(bf16[2048,3144]{0,1:T(8,128)(2,1)S(1)} %multiply_convert_fusion, bf16[3144,768]{1,0:T(8,128)(2,1)S(1)} %bitcast.36), kind=kOutput, calls=%fused_computation.42 | convolution fusion | flops 9890168832 | bytes 23998464 | tf_op jit(solution)/shard_map/dot_general | solution.py:27
  183.2 0.1 reduce-scatter.3.cloned.1.call-update
  183.2 0.0 copy-start.3
  183.2 26.7 %fusion.26 = bf16[1,2048,768]{2,1,0:T(8,128)(2,1)} fusion(bf16[1,3072,768]{2,1,0:T(8,128)(2,1)} %param.17, bf16[1,768,3072]{2,1,0:T(8,128)(2,1)} %param.16, bf16[1,2048,768]{2,1,0:T(8,128)(2,1)} %param.15), kind=kOutput, calls=%fused_computation.26 | convolution fusion | flops 19388694528 | bytes 15728640 | tf_op jit(solution)/shard_map/dot_general | solution.py:39
  210.6 15.8 %fusion.43 = f32[3144,768]{1,0:T(8,128)} fusion(bf16[2048,3144]{0,1:T(8,128)(2,1)} %copy-done, bf16[2048,768]{1,0:T(8,128)(2,1)S(1)} %copy-done.3), kind=kOutput, calls=%fused_computation.43 | convolution fusion | flops 9890168832 | bytes 25681920 | tf_op jit(solution)/shard_map/tv,td->vd/dot_general | solution.py:29
  226.5 17.9 %add_convert_fusion = bf16[3144,768]{1,0:T(8,128)(2,1)} fusion(f32[3144,768]{1,0:T(8,128)} %fusion.43, bf16[2048,768]{1,0:T(8,128)(2,1)} %all-gather.5.cloned.1.call-done, s32[2048]{0:T(1024)S(1)} %get-tuple-element.10), kind=kOutput, calls=%fused_computation.19 | convolution fusion | flops 9903851520 | bytes 17641472 | tf_op jit(solution)/shard_map/tv,td->vd/dot_general | solution.py:31
  244.4 2.4 reduce-scatter.3.cloned.1.call-done
  (11 shorter events, 0.1 us)
Async XLA Ops:
  7.2 45.0 %all-gather.3.cloned.1.call-start = ((), (), s32[]{:S(2)}) async-start(), calls=%async_computation.2 | async-start | bytes 3342336 | tf_op jit(solution)/shard_map/all_gather | solution.py:13
  8.0 218.5 %all-gather.5.cloned.1.call-start = ((), (), s32[]{:S(2)}) async-start(), calls=%async_computation.4 | async-start | bytes 3342336 | tf_op jit(solution)/shard_map/all_gather | solution.py:14
  8.8 235.6 %reduce-scatter.5.cloned.1.call-start = ((), (), s32[]{:S(2)}) async-start(), calls=%async_computation.5 | async-start | bytes 3342336 | tf_op jit(solution)/shard_map/reduce_scatter | solution.py:37
  21.0 2.3 copy-start.2
  23.2 223.6 %reduce-scatter.3.cloned.1.call-start = ((), (), s32[]{:S(2)}) async-start(), calls=%async_computation.3 | async-start | bytes 6684672 | tf_op jit(solution)/shard_map/reduce_scatter | solution.py:28
  94.6 56.7 %copy-start.1 = (s32[2048]{0:T(1024)S(1)}, s32[2048]{0:T(1024)}, u32[]{:S(2)}) copy-start(s32[2048]{0:T(1024)} %param.12) | copy-start | bytes 24580
  94.6 75.2 %slice-start = ((s8[4829184]{0:T(1024)(128)(4,1)}), s8[634880]{0:T(1024)(128)(4,1)S(1)}, s32[]{:S(2)}) async-start(s8[4829184]{0:T(1024)(128)(4,1)} %bitcast.35), calls=%async_computation.6 | async-start | bytes 1269760
  152.6 17.2 %slice-start.1 = ((s8[4829184]{0:T(1024)(128)(4,1)}), s8[4194304]{0:T(1024)(128)(4,1)S(1)}, s32[]{:S(2)}) async-start(s8[4829184]{0:T(1024)(128)(4,1)} %bitcast.35), calls=%async_computation.7 | async-start | bytes 8388608
  165.2 4.6 %copy-start = (bf16[2048,3144]{0,1:T(8,128)(2,1)}, bf16[2048,3144]{0,1:T(8,128)(2,1)S(1)}, u32[]{:S(2)}) copy-start(bf16[2048,3144]{0,1:T(8,128)(2,1)S(1)} %multiply_convert_fusion) | copy-start | bytes 38633476
  183.2 27.4 %copy-start.3 = (bf16[2048,768]{1,0:T(8,128)(2,1)S(1)}, bf16[2048,768]{1,0:T(8,128)(2,1)}, u32[]{:S(2)}) copy-start(bf16[2048,768]{1,0:T(8,128)(2,1)} %all-gather.3.cloned.1.call-done) | copy-start | bytes 9437188
Sparse Core Ops, SparseCore 0:
  9.6 42.5 all-gather.2
  53.8 35.7 all-gather.4
  92.6 53.3 reduce-scatter.4
  183.4 63.3 reduce-scatter.2
where the time goes:
time: 257 us; the launch traced here: 254 us
  matrix products  91.8 us (36%)
  blocking collectives  69.2 us (27%)
  waiting for transfers between devices  32.9 us (13%)
  other arithmetic  28 us (11%)
  between operations  16.4 us (6%)
  local copies, waits for them, and re-layouts  16.1 us (6%)
    psum x1, blocking collectives, local_step(): lax.psum(jnp.stack([jnp.sum(exp_logits, axis=1), jnp.sum(jnp.where(label_...  44.7 us
    all_gather x1, waiting for transfers between devices, local_step(): x_full = lax.all_gather(x_rows, 'pp', axis=0, tiled=True)  28.9 us
    dot_general x1, matrix products, local_step(): jnp.dot(hidden, w_down[0], preferred_element_type=jnp.float32)  26.7 us
    pmax x1, blocking collectives, local_step(): row_max = lax.pmax(jnp.max(logits, axis=1), 'pp')  24.4 us
    dot_general x1, matrix products, local_step(): jnp.einsum('tv,td->vd', id_hit, d_full, preferred_element_type=jnp.float32)  17.9 us
    dot_general x1, matrix products, local_step(): jnp.einsum('td,vd->tv', x_full, w_slice, preferred_element_type=jnp.float32)  17.9 us
    dot_general x1, matrix products, local_step(): jnp.einsum('tv,td->vd', grad_logits, x_full, preferred_element_type=jnp.f...  15.8 us
    dot_general x1, matrix products, local_step(): d_part = jnp.dot(grad_logits, w_slice, preferred_element_type=jnp.float32)  13.4 us
  transfers between devices with their start and end apart: 4, of which 2 were waited for; matrix products, arithmetic and copies ran while one was open for 52% of the time, Pallas kernels for 0%

commit v1 on v0

v1 whole, which is shorter than its diff:
```python
import functools
import math

import jax
import jax.numpy as jnp
from jax import lax
from jax.experimental import pallas as pl
from jax.experimental.pallas import tpu as pltpu
from jax.sharding import PartitionSpec as P

MESH = pl.DeviceIdType.MESH
F32 = jnp.float32
BF16 = jnp.bfloat16
QT = 640
WT = 160
NEG = -1e30


def body(
    n, vocab, emb_scale,
    x_in, d_in, w_hbm, lab_ref, ids_ref, mask_ref, act_hbm, w1_hbm, w2_hbm, emb_hbm,
    dx_out, dw_hbm, h0_out, y_hbm, loss_out,
    wv, wt, xg, dg, dxo, dxp, dxr, ho, hp, hr, stat_rx, tp_rx, stat_tx, tp_tx, mst, scale, wgt,
    x_ss, x_rs, x_ps, x_pr, d_ss, d_rs, d_ps, d_pr,
    r_ss, r_rs, r_ps, r_pr, h_ss, h_rs, h_ps, h_pr, st_ss, st_rs, tp_ss, tp_rs, loc, e_sem,
):
    ring = n // 2
    hb, dim = x_in.shape
    half = hb // 2
    tb = 2 * hb
    dhalf = dim // 2
    vpad = wv.shape[0]
    nq = vpad // QT
    nw = vpad // WT
    me = lax.axis_index("pp")
    j = me // 2
    c = lax.rem(me, 2)
    oc = 1 - c
    chip = lambda k: lax.rem(j + k + 2 * ring, ring)
    core = lambda k: {"pp": 2 * chip(k) + c}
    partner = {"pp": 2 * j + oc}
    FAR = (0, 1)
    SIGN = (1, -1)

    wv[vpad - 64:, :] = jnp.zeros((64, dim), BF16)
    w_load = pltpu.make_async_copy(w_hbm, wv.at[pl.ds(0, vocab)], loc.at[0])
    w_load.start()

    barrier = pltpu.get_barrier_semaphore()
    for p in range(1, n):
        pl.semaphore_signal(barrier, inc=1, device_id={"pp": lax.rem(me + p, n)}, device_id_type=MESH)
    pl.semaphore_wait(barrier, n - 1)

    def remote(src, dst, ss, rs, dev):
        return pltpu.make_async_remote_copy(src_ref=src, dst_ref=dst, send_sem=ss, recv_sem=rs, device_id=dev, device_id_type=MESH)

    def gather_flow(src, buf, ss, rs, ps, pr):
        def rows(origin, cc, h):
            return buf.at[pl.ds(pl.multiple_of(origin * tb + cc * hb + h * half, half), half)]

        def send(d, s, h):
            origin = chip(-SIGN[d] * s)
            ref = src.at[pl.ds(h * half, half)] if s == 0 else rows(origin, c, h)
            return remote(ref, rows(origin, c, h), ss.at[d, s, h], rs.at[d, s, h], core(SIGN[d]))

        def share(d, s, h):
            origin = chip(-SIGN[d] * (s + 1))
            return remote(rows(origin, c, h), rows(origin, c, h), ps.at[d, s, h], pr.at[d, s, h], partner)

        def share_in(d, s, h):
            origin = chip(-SIGN[d] * (s + 1))
            return remote(rows(origin, oc, h), rows(origin, oc, h), ps.at[d, s, h], pr.at[d, s, h], partner)

        def own():
            mine = buf.at[pl.ds(pl.multiple_of(j * tb + c * hb, hb), hb)]
            return remote(src, mine, ps.at[0, 3, 1], pr.at[0, 3, 1], partner)

        def start():
            for k in range(2):
                for d in range(2):
                    send(d, 0, FAR[d] if k == 0 else 1 - FAR[d]).start()
            own().start()
            buf[pl.ds(pl.multiple_of(j * tb + c * hb, hb), hb), :] = src[...]

        units = [(s, k) for s in range(4) for k in range(2) if s < 3 or k == 0]

        def event(e):
            s, k = units[e]
            for d in range(2):
                h = FAR[d] if k == 0 else 1 - FAR[d]
                send(d, s, h).wait_recv()
                if s < 2 or (s == 2 and k == 0):
                    send(d, s + 1, h).start()
                share(d, s, h).start()

        def finish():
            for s, k in units:
                for d in range(2):
                    h = FAR[d] if k == 0 else 1 - FAR[d]
                    share_in(d, s, h).wait_recv()
            own().wait_recv()

        def drain():
            for s, k in units:
                for d in range(2):
                    h = FAR[d] if k == 0 else 1 - FAR[d]
                    send(d, s, h).wait_send()
                    share(d, s, h).wait_send()
            own().wait_send()

        return start, event, finish, drain, len(units)

    def scatter_flow(away, own, pbuf, rx, ss, rs, ps, pr, length):
        def share(b, k):
            return remote(away(b, oc), pbuf.at[b], ps.at[k], pr.at[k], partner)

        def part(ref, h):
            return ref.at[pl.ds(h * length, length)]

        def send(d, k, h):
            return remote(part(rx.at[d, k], h), part(rx.at[d, k - 1], h), ss.at[d, k, h], rs.at[d, k - 1, h], core(SIGN[d]))

        def emit(d, k, far, first):
            h = FAR[d] if far else 1 - FAR[d]
            b = chip(SIGN[d] * k)
            if first:
                part(rx.at[d, k], h)[...] = part(own(b), h)[...] + part(pbuf.at[b], h)[...]
            else:
                send(d, k + 1, h).wait_recv()
                part(rx.at[d, k], h)[...] = part(rx.at[d, k], h)[...] + (part(own(b), h)[...] + part(pbuf.at[b], h)[...])
            send(d, k, h).start()

        def final(out):
            for far in (False, True):
                for d in range(2):
                    send(d, 1, FAR[d] if far else 1 - FAR[d]).wait_recv()
            out[...] = (own(j)[...] + pbuf[j]) + (rx[0, 0] + rx[1, 0])

        def drain():
            for d in range(2):
                for k, far in ((4, True), (3, False), (3, True), (2, False), (2, True), (1, False), (1, True)):
                    send(d, k, FAR[d] if far else 1 - FAR[d]).wait_send()

        return share, emit, final, drain

    x_start, x_event, x_finish, x_drain, n_units = gather_flow(x_in, xg, x_ss, x_rs, x_ps, x_pr)
    d_start, d_event, d_finish, d_drain, _ = gather_flow(d_in, dg, d_ss, d_rs, d_ps, d_pr)
    h_share, h_emit, h_final, h_drain = scatter_flow(
        lambda b, cc: emb_hbm.at[pl.ds(pl.multiple_of(b * tb + cc * hb, hb), hb)], lambda b: ho.at[b], hp, hr, h_ss, h_rs, h_ps, h_pr, half)
    r_share, r_emit, r_final, r_drain = scatter_flow(
        lambda b, cc: dxo.at[b, cc], lambda b: dxo.at[b, c], dxp, dxr, r_ss, r_rs, r_ps, r_pr, dhalf)

    x_start()
    for k in range(ring):
        h_share(lax.rem(j + k, ring), k).start()

    def e_load(b):
        return pltpu.make_async_copy(emb_hbm.at[pl.ds(pl.multiple_of(b * tb + c * hb, hb), hb)], ho.at[b], e_sem.at[b])

    for b in range(ring):
        e_load(b).start()

    def h_partner_wait():
        for k in range(ring):
            h_share(lax.rem(j + k, ring), k).wait_recv()
            e_load(k).wait()

    def h_both(k, far, first):
        for d in range(2):
            h_emit(d, k, far, first)

    def h_init():
        h_partner_wait()
        h_both(4, True, True)
        h_both(3, False, True)

    side = [
        h_init, d_start,
        lambda: h_both(3, True, False), lambda: d_event(0),
        lambda: h_both(2, False, False), lambda: d_event(1),
        lambda: h_both(2, True, False), lambda: d_event(2),
        lambda: h_both(1, False, False), lambda: d_event(3),
        lambda: h_both(1, True, False), lambda: d_event(4),
        lambda: d_event(5), lambda: d_event(6),
    ]

    def at(index, table):
        for when, todo in table:
            pl.when(index == when)(todo)

    chunk = tb
    n_chunks = act_hbm.shape[0] // chunk
    hid = w1_hbm.shape[1]

    w_load.wait()

    @pl.loop(0, vpad // 128)
    def _(t):
        o = pl.multiple_of(t * 128, 128)
        wt[:, pl.ds(o, 128)] = wv[pl.ds(o, 128), :].T

    def mlp(w1v, w2v, abuf, ybuf, hbuf, wsem, asem, ysem):
        c1 = pltpu.make_async_copy(w1_hbm, w1v, wsem.at[0])
        c2 = pltpu.make_async_copy(w2_hbm, w2v, wsem.at[1])
        c1.start()
        c2.start()

        def a_copy(i):
            slot = lax.rem(i, 2)
            return pltpu.make_async_copy(act_hbm.at[pl.ds(pl.multiple_of(i * chunk, chunk), chunk)], abuf.at[slot], asem.at[slot])

        def y_copy(i):
            slot = lax.rem(i, 2)
            return pltpu.make_async_copy(ybuf.at[slot], y_hbm.at[pl.ds(pl.multiple_of(i * chunk, chunk), chunk)], ysem.at[slot])

        a_copy(0).start()
        c1.wait()
        c2.wait()
        first = [(2, lambda: x_event(1)), (3, lambda: x_event(2)), (4, lambda: x_event(4)), (5, lambda: x_event(5)), (6, side[0]), (7, side[1])]
        second = [(1, lambda: x_event(0)), (3, lambda: x_event(3)), (5, lambda: x_event(6)), (7, side[2])]

        @pl.loop(0, n_chunks)
        def _(i):
            slot = lax.rem(i, 2)
            a_copy(i).wait()

            @pl.when(i + 1 < n_chunks)
            def _():
                a_copy(i + 1).start()

            a = abuf[slot]
            step = min(512, hid)
            for t in range(hid // step):
                up = jnp.dot(a, w1v[:, t * step:(t + 1) * step], preferred_element_type=F32)
                hbuf[:, t * step:(t + 1) * step] = jax.nn.gelu(up).astype(BF16)
            at(i, first)

            @pl.when(i >= 2)
            def _():
                y_copy(i - 2).wait()

            ybuf[slot] = (abuf[slot].astype(F32) + jnp.dot(hbuf[...], w2v[...], preferred_element_type=F32)).astype(BF16)
            y_copy(i).start()
            at(i, second)

        y_copy(n_chunks - 2).wait()
        y_copy(n_chunks - 1).wait()

    pl.run_scoped(
        mlp,
        pltpu.VMEM(w1_hbm.shape, BF16), pltpu.VMEM(w2_hbm.shape, BF16),
        pltpu.VMEM((2, chunk, dim), BF16), pltpu.VMEM((2, chunk, dim), BF16), pltpu.VMEM((chunk, hid), BF16),
        pltpu.SemaphoreType.DMA((2,)), pltpu.SemaphoreType.DMA((2,)), pltpu.SemaphoreType.DMA((2,)),
    )

    def head(z):
        x_finish()
        kept = mask_ref[...]
        count = jnp.maximum(jnp.sum(kept, keepdims=True), 1.0)
        wgt[...] = kept / count

        def row_iota(rows):
            return lax.broadcasted_iota(jnp.int32, (rows, tb), 0)

        @pl.loop(0, ring)
        def _(b):
            xb = xg[pl.ds(pl.multiple_of(b * tb, tb), tb), :]
            lab = lab_ref[pl.ds(b, 1), :]
            tops, sums, tgt = [], [], jnp.zeros((1, tb), F32)
            def logits(q):
                zt = lax.dot_general(wv[q * QT:(q + 1) * QT, :], xb, (((1,), (1,)), ((), ())), preferred_element_type=F32)
                if (q + 1) * QT > vocab:
                    zt = jnp.where(row_iota(QT) + q * QT < vocab, zt, NEG)
                z[b, q * QT:(q + 1) * QT, :] = zt

            logits(0)
            for q in range(nq):
                if q + 1 < nq:
                    logits(q + 1)
                part = z.at[b, pl.ds(q * QT, QT)]
                top = jnp.max(part[...], axis=0, keepdims=True)
                zt = part[...]
                e = jnp.exp(zt - top)
                part[...] = e
                tgt = tgt + jnp.sum(jnp.where(row_iota(QT) + q * QT == lab, zt, 0.0), axis=0, keepdims=True)
                sums.append(jnp.sum(e, axis=0, keepdims=True))
                tops.append(top)
                mst[q, pl.ds(b, 1), :] = top
            peak = functools.reduce(jnp.maximum, tops)
            total = sum(s * jnp.exp(t - peak) for s, t in zip(sums, tops))
            stat_tx[pl.ds(b, 1), :] = peak + jnp.log(total)
            tp_tx[pl.ds(b, 1), :] = tgt * mask_ref[pl.ds(b, 1), :]
            at(b, [(k, side[3 + k]) for k in range(8)])

        def stat_copy(p):
            return remote(stat_tx, stat_rx.at[me], st_ss.at[p], st_rs.at[p], {"pp": lax.rem(me + p, n)})

        def tp_copy(p):
            return remote(tp_rx.at[pl.ds(n, 1)], tp_rx.at[pl.ds(me, 1)], tp_ss.at[p], tp_rs.at[p], {"pp": lax.rem(me + p, n)})

        order = [n // 2] + [q for k in range(1, n // 2) for q in (n // 2 - k, n // 2 + k)]
        for p in order:
            stat_copy(p).start()
        stat_rx[me] = stat_tx[...]
        mine = jnp.sum(tp_tx[...], keepdims=True)
        tp_rx[pl.ds(n, 1), :] = jnp.broadcast_to(mine, (1, 128))
        tp_rx[pl.ds(me, 1), :] = jnp.broadcast_to(mine, (1, 128))
        for p in order:
            tp_copy(p).start()
        for p in range(1, n):
            stat_copy(p).wait_recv()
        peak = stat_rx[0]
        for p in range(1, n):
            peak = jnp.maximum(peak, stat_rx[p])
        total = jnp.exp(stat_rx[0] - peak)
        for p in range(1, n):
            total = total + jnp.exp(stat_rx[p] - peak)
        lse = peak + jnp.log(total)
        for q in range(nq):
            scale[q] = jnp.exp(mst[q] - lse) * wgt[...]
        lse_sum = jnp.sum(kept * lse, keepdims=True)

        def r_both(k, far, first):
            for d in range(2):
                r_emit(d, k, far, first)

        def dest(t):
            k = jnp.where(t == 0, 4, 3 - (t - 1) // 2)
            k = jnp.where(t == 0, 4, k * (1 - 2 * lax.rem(jnp.maximum(t - 1, 0), 2)))
            return chip(k)

        def pw(t):
            r_share(dest(t), t).wait_recv()

        def first_4():
            pw(0)
            r_both(4, True, True)

        def first_3r():
            pw(1)
            r_emit(0, 3, False, True)

        def first_3l():
            pw(2)
            r_emit(1, 3, False, True)

        def acc_2():
            pw(3)
            pw(4)
            r_both(2, False, False)

        dx_events = [
            (1, first_4), (2, first_3r), (3, first_3l), (4, lambda: r_both(3, True, False)),
            (6, acc_2), (7, lambda: r_both(2, True, False)),
        ]
        dx_side = [(0, side[11]), (1, side[12]), (3, side[13]), (5, lambda: h_final(h0_out))]

        def blocks(gbuf):
            @pl.loop(0, ring)
            def _(t):
                b = dest(t)
                lab = lab_ref[pl.ds(b, 1), :]
                wrow = wgt[pl.ds(b, 1), :]
                for q in range(nq):
                    g = z[b, q * QT:(q + 1) * QT, :] * scale[q, pl.ds(b, 1), :]
                    g = g - jnp.where(row_iota(QT) + q * QT == lab, wrow, 0.0)
                    gbuf[q * QT:(q + 1) * QT, :] = g.astype(BF16)
                @pl.loop(0, dim // 256)
                def _(m):
                    o = pl.multiple_of(m * 256, 256)
                    res = jnp.dot(wt[pl.ds(o, 256), :], gbuf[...], preferred_element_type=F32)
                    dxo[b, 0, pl.ds(o, 256), :] = res[:, :hb]
                    dxo[b, 1, pl.ds(o, 256), :] = res[:, hb:]

                r_share(b, t).start()
                at(t, dx_events)
                at(t, dx_side)

        pl.run_scoped(blocks, pltpu.VMEM((vpad, tb), BF16))
        def tables(gt, ht, wbuf, wsem):
            def w_copy(i, rows):
                slot = lax.rem(i, 2)
                return pltpu.make_async_copy(wbuf.at[slot, pl.ds(0, rows)], dw_hbm.at[pl.ds(pl.multiple_of(i * WT, 8), rows)], wsem.at[slot])

            tail = vocab - (nw - 1) * WT

            def acc_1():
                pw(5)
                pw(6)
                r_both(1, False, False)

            dw_events = [(2, acc_1), (7, lambda: r_both(1, True, False))]

            @pl.loop(0, nw)
            def _(i):
                o = pl.multiple_of(i * WT, WT)
                q = i // (QT // WT)
                slot = lax.rem(i, 2)
                rid = row_iota(WT) + i * WT
                for b in range(ring):
                    g = z[b, pl.ds(o, WT), :] * scale[q, b:b + 1, :]
                    g = g - jnp.where(rid == lab_ref[b:b + 1, :], wgt[b:b + 1, :], 0.0)
                    gt[:, b * tb:(b + 1) * tb] = g.astype(BF16)
                    ht[:, b * tb:(b + 1) * tb] = jnp.where(rid == ids_ref[b:b + 1, :], 1.0, 0.0).astype(BF16)
                @pl.when(i >= 2)
                def _():
                    w_copy(i - 2, WT).wait()

                for t in range(dim // 256):
                    cols = slice(t * 256, (t + 1) * 256)
                    head_part = jnp.dot(gt[...], xg[:, cols], preferred_element_type=F32)
                    table_part = jnp.dot(ht[...], dg[:, cols], preferred_element_type=F32)
                    wbuf[slot, :, cols] = (head_part + table_part * emb_scale).astype(BF16)

                @pl.when(i < nw - 1)
                def _():
                    w_copy(i, WT).start()

                at(i, dw_events)

            w_copy(nw - 1, tail).start()
            w_copy(nw - 2, WT).wait()
            w_copy(nw - 1, tail).wait()

        d_finish()
        pl.run_scoped(
            tables,
            pltpu.VMEM((WT, ring * tb), BF16), pltpu.VMEM((WT, ring * tb), BF16),
            pltpu.VMEM((2, WT, dim), BF16), pltpu.SemaphoreType.DMA((2,)),
        )
        pw(7)
        r_final(dx_out)
        for p in range(1, n):
            tp_copy(p).wait_recv()
        target = jnp.sum(tp_rx[0:n, :], axis=0, keepdims=True)
        loss_out[...] = jnp.broadcast_to((lse_sum - target) / count, loss_out.shape)
        for p in range(1, n):
            stat_copy(p).wait_send()
            tp_copy(p).wait_send()
        for t in range(ring):
            r_share(dest(jnp.int32(t)), t).wait_send()

    pl.run_scoped(
        head,
        pltpu.VMEM((ring, vpad, tb), F32),
    )
    x_drain()
    d_drain()
    r_drain()
    h_drain()
    for k in range(ring):
        h_share(lax.rem(j + k, ring), k).wait_send()


def solution(mesh):
    n = mesh.shape["pp"]
    ring = n // 2

    def local_step(x_rows, w_slice, labels, tok_mask, next_ids, d_rows, act_in, w_up, w_down):
        vocab, dim = w_slice.shape
        hb = x_rows.shape[0]
        tb = 2 * hb
        vpad = -(-vocab // QT) * QT
        emb_scale = math.sqrt(dim)
        offset = lax.axis_index("pp") * vocab
        lab = labels - offset
        lab = jnp.where((lab >= 0) & (lab < vocab), lab, -1).reshape(ring, tb)
        pos = next_ids - offset
        mask = tok_mask.astype(F32).reshape(ring, tb)
        in_share = (pos >= 0) & (pos < vocab)
        picked = w_slice[jnp.clip(pos, 0, vocab - 1)]
        emb = jnp.where(in_share[:, None], picked.astype(F32) * emb_scale, 0.0).astype(BF16)
        vmem = pl.BlockSpec(memory_space=pltpu.VMEM)
        hbm = pl.BlockSpec(memory_space=pltpu.HBM)
        dma = lambda *s: pltpu.SemaphoreType.DMA(s)
        dx, dw, h0, y, loss = pl.pallas_call(
            functools.partial(body, n, vocab, emb_scale),
            out_shape=[
                jax.ShapeDtypeStruct((dim, hb), F32),
                jax.ShapeDtypeStruct((vocab, dim), BF16),
                jax.ShapeDtypeStruct((hb, dim), BF16),
                jax.ShapeDtypeStruct(act_in.shape[1:], BF16),
                jax.ShapeDtypeStruct((8, 128), F32),
            ],
            in_specs=[vmem, vmem, hbm, vmem, vmem, vmem, hbm, hbm, hbm, hbm],
            out_specs=[vmem, hbm, vmem, hbm, vmem],
            scratch_shapes=[
                pltpu.VMEM((vpad, dim), BF16), pltpu.VMEM((dim, vpad), BF16),
                pltpu.VMEM((ring * tb, dim), BF16), pltpu.VMEM((ring * tb, dim), BF16),
                pltpu.VMEM((ring, 2, dim, hb), F32), pltpu.VMEM((ring, dim, hb), F32), pltpu.VMEM((2, 5, dim, hb), F32),
                pltpu.VMEM((ring, hb, dim), BF16), pltpu.VMEM((ring, hb, dim), BF16), pltpu.VMEM((2, 5, hb, dim), BF16),
                pltpu.VMEM((n, ring, tb), F32), pltpu.VMEM((n + 8, 128), F32),
                pltpu.VMEM((ring, tb), F32), pltpu.VMEM((ring, tb), F32),
                pltpu.VMEM((vpad // QT, ring, tb), F32), pltpu.VMEM((vpad // QT, ring, tb), F32), pltpu.VMEM((ring, tb), F32),
            ] + [dma(2, 4, 2)] * 8 + [dma(2, 5, 2), dma(2, 5, 2), dma(ring), dma(ring)] * 2 + [dma(n)] * 4 + [dma(1), dma(ring)],
            compiler_params=pltpu.CompilerParams(collective_id=0, has_side_effects=True, vmem_limit_bytes=67043328),
        )(x_rows, d_rows, w_slice, lab, jnp.where(in_share, pos, -1).reshape(ring, tb), mask, act_in[0], w_up[0], w_down[0], emb)
        return loss[0, :1], dx.T, dw, h0, y[None]

    token_spec = P(("dp", "pp"))
    return jax.shard_map(
        local_step,
        mesh=mesh,
        in_specs=(token_spec, P("pp"), P("dp"), P("dp"), P("dp"), token_spec, token_spec, P("pp"), P("pp")),
        out_specs=(P("dp"), token_spec, token_spec, token_spec, token_spec),
        check_vma=False,
    )
```

time: 257 us -> 160 us (0.62)
  Pallas kernels: 0 us -> 131 us
  matrix products: 91.8 us -> 0 us
  blocking collectives: 69.2 us -> 0 us
  waiting for transfers between devices: 32.9 us -> 0 us
  other arithmetic: 28 us -> 4.22 us
  between operations: 16.4 us -> 0.66 us
  local copies, waits for them, and re-layouts: 16.1 us -> 23.8 us
    pallas_call x0 -> x1, Pallas kernels: none -> 131 us  [local_step(): pl.pallas_call(functools.partial(body, n, vocab, emb_scale), out_shape=[j...]
    dot_general x5 -> x0, matrix products: 91.8 us -> none  [the longest x1 26.7 us: local_step(): jnp.dot(hidden, w_down[0], preferred_element_type=jnp.float32)]
    psum x1 -> x0, blocking collectives: 44.7 us -> none  [local_step(): lax.psum(jnp.stack([jnp.sum(exp_logits, axis=1), jnp.sum(jnp.where(label_...]
    all_gather x2 -> x0, waiting for transfers between devices: 28.9 us -> none  [the longest x1 28.9 us: local_step(): x_full = lax.all_gather(x_rows, 'pp', axis=0, tiled=True)]
    pmax x1 -> x0, blocking collectives: 24.4 us -> none  [local_step(): row_max = lax.pmax(jnp.max(logits, axis=1), 'pp')]
    reduce_sum x2 -> x0, other arithmetic: 12.5 us -> none  [the longest x1 11.9 us: local_step(): jnp.sum(exp_logits, axis=1)]
    convert_element_type x2, other arithmetic: 14.7 us -> 2.79 us  [the longest x1 2.09 us: local_step(): jnp.where(in_share[:, None], picked.astype(F32) * emb_scale, 0.0)]
    unnamed x12 -> x8, local copies, waits for them, and re-layouts: 4.63 us -> 9.31 us
  transfers between devices with their start and end apart: 4 -> 0, of which waited for: 2 -> 0; matrix products, arithmetic and copies ran while one was open for 52% -> 0% of each run, Pallas kernels for 0% -> 0%
where the time goes in v1:
time: 160 us; the launch traced here: 159 us
  Pallas kernels  131 us (82%)
  local copies, waits for them, and re-layouts  23.8 us (15%)
  other arithmetic  4.22 us (3%)
    pallas_call x1, Pallas kernels, local_step(): pl.pallas_call(functools.partial(body, n, vocab, emb_scale), out_shape=[j...  131 us
    gather x1, local copies, waits for them, and re-layouts, local_step(): picked = w_slice[jnp.clip(pos, 0, vocab - 1)]  11.4 us
    unnamed x8, local copies, waits for them, and re-layouts  9.31 us

profile of v1, /device:TPU:21, one launch (start us, length us, event | category | flops | bytes accessed | tf_op | source)
XLA Modules:
  0.0 159.3 jit_solution(15027196540977132493)
XLA Ops:
  0.6 0.7 compare_and_fusion
  1.3 0.7 convert_element_type.9
  2.0 0.6 reshape.22.mask_ref
  2.6 0.7 fusion
  3.4 0.6 reshape.21.ids_ref
  4.0 0.6 reshape.20.lab_ref
  4.6 11.4 %gather_fusion = bf16[2048,768]{1,0:T(8,128)(2,1)S(1)} fusion(bf16[3144,768]{1,0:T(8,128)(2,1)} %w_hbm.1, s32[2048]{0:T(1024)S(1)} %get-tuple-element.20), kind=kCustom, calls=%fused_computation | custom fusion | bytes 6299648 | tf_op jit(solution)/shard_map/gather | solution.py:471
  16.0 2.1 %select_convert_fusion.emb_hbm = bf16[2048,768]{1,0:T(8,128)(2,1)} fusion(bf16[2048,768]{1,0:T(8,128)(2,1)S(1)} %gather_fusion, pred[2048]{0:T(1024)(128)(4,1)S(1)} %compare_and_fusion), kind=kLoop, calls=%fused_computation.1 | loop fusion | flops 6291456 | bytes 6293504 | tf_op jit(solution)/shard_map/convert_element_type | solution.py:472
  18.1 130.7 %shard_map.128 = (f32[768,128]{1,0:T(8,128)}, bf16[3144,768]{1,0:T(8,128)(2,1)}, bf16[128,768]{1,0:T(8,128)(2,1)}, bf16[2048,768]{1,0:T(8,128)(2,1)}, f32[8,128]{1,0:T(8,128)}) custom-call(bf16[128,768]{1,0:T(8,128)(2,1)} %x_in.1, bf16[128,768]{1,0:T(8,128)(2,1)} %d_in.1, bf16[3144,768]{1,0:T(8,128)(2,1)} %w_hbm.1, s32[8,256]{1,0:T(8,128)} %reshape.20.lab_ref, ...), custom_call_target="tpu_custom_call" | custom-call | tf_op jit(solution)/shard_map/pallas_call | solution.py:476
  148.8 1.2 slice.3
  150.0 1.9 %copy.14 = f32[128,768]{1,0:T(8,128)} copy(f32[128,768]{0,1:T(8,128)} %bitcast.10) | data formatting | bytes 786432
  151.9 0.0 copy-start.1
  151.9 0.0 copy-start
  151.9 5.0 %copy.18 = bf16[3144,768]{1,0:T(8,128)(2,1)} copy(bf16[3144,768]{1,0:T(8,128)(2,1)} %get-tuple-element.30) | data formatting | bytes 9658368
  157.0 0.0 copy-done.1
  157.0 0.7 copy.19
  157.6 0.0 copy-done
  157.6 1.7 %copy.20 = bf16[1,2048,768]{2,1,0:T(8,128)(2,1)} copy(bf16[1,2048,768]{2,1,0:T(8,128)(2,1)S(1)} %bitcast.8) | data formatting | bytes 6291456
Async XLA Ops:
  151.9 5.1 %copy-start.1 = (bf16[128,768]{1,0:T(8,128)(2,1)S(1)}, bf16[128,768]{1,0:T(8,128)(2,1)}, u32[]{:S(2)}) copy-start(bf16[128,768]{1,0:T(8,128)(2,1)} %get-tuple-element.31) | copy-start | bytes 589828
  151.9 5.7 %copy-start = (bf16[2048,768]{1,0:T(8,128)(2,1)S(1)}, bf16[2048,768]{1,0:T(8,128)(2,1)}, u32[]{:S(2)}) copy-start(bf16[2048,768]{1,0:T(8,128)(2,1)} %get-tuple-element.14) | copy-start | bytes 9437188

commit v2 on v1

v2 whole, which is shorter than its diff:
```python
import functools
import math

import jax
import jax.numpy as jnp
from jax import lax
from jax.experimental import pallas as pl
from jax.experimental.pallas import tpu as pltpu
from jax.sharding import PartitionSpec as P

MESH = pl.DeviceIdType.MESH
F32 = jnp.float32
BF16 = jnp.bfloat16
QT = 320
WT = 320
NEG = -1e30
OUTER, INNER = True, False
FIRST, LATER = True, False
NT = (((1,), (1,)), ((), ()))
TN = (((0,), (0,)), ((), ()))
ALL = ...
PICK = 256


def down(x):
    return jnp.sum(x, axis=0, keepdims=True)


def body(
    n, vocab,
    x_in, d_in, w_hbm, lab_ref, mask_ref, act_hbm, w1_hbm, w2_hbm, emb_hbm,
    dx_out, dw_hbm, h0_out, y_hbm, loss_out, dg_hbm,
    wv, wt, xg, dxo, dxp, dxr, ho, hp, hr, stat_rx, tp_rx, stat_tx, tp_tx, mst, scale, wgt,
    x_ss, x_rs, x_ps, x_pr, d_ss, d_rs, d_ps, d_pr,
    r_ss, r_rs, r_ps, r_pr, h_ss, h_rs, h_ps, h_pr, st_ss, st_rs, tp_ss, tp_rs, loc, e_sem,
):
    ring = n // 2
    hb, dim = x_in.shape
    half = hb // 2
    tb = 2 * hb
    dhalf = dim // 2
    vpad = wv.shape[0]
    nq = vpad // QT
    nw = vpad // WT
    me = lax.axis_index("pp")
    j = me // 2
    c = lax.rem(me, 2)
    oc = 1 - c
    chip = lambda k: lax.rem(j + k + 2 * ring, ring)
    core = lambda k: {"pp": 2 * chip(k) + c}
    partner = {"pp": 2 * j + oc}
    FAR = (0, 1)
    SIGN = (1, -1)

    wv[vpad - 64:, :] = jnp.zeros((64, dim), BF16)
    w_load = pltpu.make_async_copy(w_hbm, wv.at[pl.ds(0, vocab)], loc.at[0])

    barrier = pltpu.get_barrier_semaphore()
    for p in range(1, n):
        pl.semaphore_signal(barrier, inc=1, device_id={"pp": lax.rem(me + p, n)}, device_id_type=MESH)

    def remote(src, dst, ss, rs, dev):
        return pltpu.make_async_remote_copy(src_ref=src, dst_ref=dst, send_sem=ss, recv_sem=rs, device_id=dev, device_id_type=MESH)

    def gather_flow(src, buf, ss, rs, ps, pr, keep_sem=None):
        def rows(origin, cc, h):
            return buf.at[pl.ds(pl.multiple_of(origin * tb + cc * hb + h * half, half), half)]

        def send(d, s, h):
            origin = chip(-SIGN[d] * s)
            ref = src.at[pl.ds(h * half, half)] if s == 0 else rows(origin, c, h)
            return remote(ref, rows(origin, c, h), ss.at[d, s, h], rs.at[d, s, h], core(SIGN[d]))

        def share(d, s, h):
            origin = chip(-SIGN[d] * (s + 1))
            return remote(rows(origin, c, h), rows(origin, c, h), ps.at[d, s, h], pr.at[d, s, h], partner)

        def share_in(d, s, h):
            origin = chip(-SIGN[d] * (s + 1))
            return remote(rows(origin, oc, h), rows(origin, oc, h), ps.at[d, s, h], pr.at[d, s, h], partner)

        def own():
            mine = buf.at[pl.ds(pl.multiple_of(j * tb + c * hb, hb), hb)]
            return remote(src, mine, ps.at[0, 3, 1], pr.at[0, 3, 1], partner)

        def keep():
            return pltpu.make_async_copy(src, buf.at[pl.ds(pl.multiple_of(j * tb + c * hb, hb), hb)], keep_sem)

        def start():
            for k in range(2):
                for d in range(2):
                    send(d, 0, FAR[d] if k == 0 else 1 - FAR[d]).start()
            own().start()
            if keep_sem is None:
                buf[pl.ds(pl.multiple_of(j * tb + c * hb, hb), hb), :] = src[...]
            else:
                keep().start()

        units = [(s, k) for s in range(4) for k in range(2) if s < 3 or k == 0]

        def event(e):
            s, k = units[e]
            for d in range(2):
                h = FAR[d] if k == 0 else 1 - FAR[d]
                send(d, s, h).wait_recv()
                if s < 2 or (s == 2 and k == 0):
                    send(d, s + 1, h).start()
                share(d, s, h).start()

        def finish():
            for s, k in units:
                for d in range(2):
                    h = FAR[d] if k == 0 else 1 - FAR[d]
                    share_in(d, s, h).wait_recv()
            own().wait_recv()

        def drain():
            for s, k in units:
                for d in range(2):
                    h = FAR[d] if k == 0 else 1 - FAR[d]
                    send(d, s, h).wait_send()
                    share(d, s, h).wait_send()
            own().wait_send()
            if keep_sem is not None:
                keep().wait()

        return start, event, finish, drain, len(units)

    def scatter_flow(away, own, pbuf, rx, ss, rs, ps, pr, length):
        def share(b, k):
            return remote(away(b, oc), pbuf.at[b], ps.at[k], pr.at[k], partner)

        def part(ref, h):
            return ref.at[pl.ds(h * length, length)]

        def send(d, k, h):
            return remote(part(rx.at[d, k], h), part(rx.at[d, k - 1], h), ss.at[d, k, h], rs.at[d, k - 1, h], core(SIGN[d]))

        def emit(d, k, far, first):
            h = FAR[d] if far else 1 - FAR[d]
            b = chip(SIGN[d] * k)
            if first:
                part(rx.at[d, k], h)[...] = part(own(b), h)[...] + part(pbuf.at[b], h)[...]
            else:
                send(d, k + 1, h).wait_recv()
                part(rx.at[d, k], h)[...] = part(rx.at[d, k], h)[...] + (part(own(b), h)[...] + part(pbuf.at[b], h)[...])
            send(d, k, h).start()

        def final(out):
            for far in (INNER, OUTER):
                for d in range(2):
                    send(d, 1, FAR[d] if far else 1 - FAR[d]).wait_recv()
            out[...] = (own(j)[...] + pbuf[j]) + (rx[0, 0] + rx[1, 0])

        def drain():
            for d in range(2):
                for k, far in ((4, OUTER), (3, INNER), (3, OUTER), (2, INNER), (2, OUTER), (1, INNER), (1, OUTER)):
                    send(d, k, FAR[d] if far else 1 - FAR[d]).wait_send()

        return share, emit, final, drain

    x_start, x_event, x_finish, x_drain, n_units = gather_flow(x_in, xg, x_ss, x_rs, x_ps, x_pr)
    d_start, d_event, d_finish, d_drain, _ = gather_flow(d_in, dg_hbm, d_ss, d_rs, d_ps, d_pr, loc.at[1])
    h_share, h_emit, h_final, h_drain = scatter_flow(
        lambda b, cc: emb_hbm.at[pl.ds(pl.multiple_of(b * tb + cc * hb, hb), hb)], lambda b: ho.at[b], hp, hr, h_ss, h_rs, h_ps, h_pr, half)
    r_share, r_emit, r_final, r_drain = scatter_flow(
        lambda b, cc: dxo.at[b, cc], lambda b: dxo.at[b, c], dxp, dxr, r_ss, r_rs, r_ps, r_pr, dhalf)

    def e_load(b):
        return pltpu.make_async_copy(emb_hbm.at[pl.ds(pl.multiple_of(b * tb + c * hb, hb), hb)], ho.at[b], e_sem.at[b])

    def enter():
        pl.semaphore_wait(barrier, n - 1)
        x_start()
        for k in range(ring):
            h_share(lax.rem(j + k, ring), k).start()

    def h_partner_wait():
        for k in range(ring):
            h_share(lax.rem(j + k, ring), k).wait_recv()
            e_load(k).wait()

    def h_both(k, far, first):
        for d in range(2):
            h_emit(d, k, far, first)

    def h_init():
        h_partner_wait()
        h_both(4, OUTER, FIRST)
        h_both(3, INNER, FIRST)

    side = [
        h_init, d_start,
        lambda: h_both(3, OUTER, LATER), lambda: d_event(0),
        lambda: h_both(2, INNER, LATER), lambda: d_event(1),
        lambda: h_both(2, OUTER, LATER), lambda: d_event(2),
        lambda: h_both(1, INNER, LATER), lambda: d_event(3),
        lambda: h_both(1, OUTER, LATER), lambda: d_event(4),
        lambda: d_event(5), lambda: d_event(6),
    ]

    def at(index, table):
        for when, todo in table:
            def run(when=when, todo=todo):
                with jax.named_scope(f"ev{when}"):
                    todo()

            pl.when(index == when)(run)

    chunk = act_hbm.shape[0] // 4
    n_chunks = act_hbm.shape[0] // chunk
    hid = w1_hbm.shape[1]

    def mlp(w1v, w2v, abuf, ybuf, hbuf, wsem, asem, ysem):
        c1 = pltpu.make_async_copy(w1_hbm, w1v, wsem.at[0])
        c2 = pltpu.make_async_copy(w2_hbm, w2v, wsem.at[1])
        c1.start()

        def a_copy(i):
            slot = lax.rem(i, 2)
            return pltpu.make_async_copy(act_hbm.at[pl.ds(pl.multiple_of(i * chunk, chunk), chunk)], abuf.at[slot], asem.at[slot])

        a_copy(0).start()

        def y_copy(i):
            slot = lax.rem(i, 2)
            return pltpu.make_async_copy(ybuf.at[slot], y_hbm.at[pl.ds(pl.multiple_of(i * chunk, chunk), chunk)], ysem.at[slot])

        c1.wait()
        c2.start()
        w_load.start()
        for b in range(ring):
            e_load(b).start()
        first = [(0, enter), (1, lambda: x_event(1)), (2, lambda: x_event(4)), (3, side[1])]
        second = [(1, lambda: x_event(2)), (2, lambda: x_event(5)), (3, lambda: x_event(6))]
        third = [(0, lambda: x_event(0)), (1, lambda: x_event(3)), (2, side[0]), (3, side[2])]

        @pl.loop(0, n_chunks)
        def _(i):
            slot = lax.rem(i, 2)
            a_copy(i).wait()

            @pl.when(i + 1 < n_chunks)
            def _():
                a_copy(i + 1).start()

            step = min(512, hid // 2)
            per = hid // step

            def up(lo, hi):
                for t in range(lo, hi):
                    u = jnp.dot(abuf[slot], w1v[:, t * step:(t + 1) * step], preferred_element_type=F32)
                    hbuf[:, t * step:(t + 1) * step] = jax.nn.gelu(u).astype(BF16)

            up(0, per // 2)
            at(i, first)
            up(per // 2, per)
            at(i, second)

            @pl.when(i == 0)
            def _():
                c2.wait()

            @pl.when(i >= 2)
            def _():
                y_copy(i - 2).wait()

            for t in range(dim // 256):
                cols = slice(t * 256, (t + 1) * 256)
                low = jnp.dot(hbuf[...], w2v[:, cols], preferred_element_type=F32)
                ybuf[slot, :, cols] = (abuf[slot, :, cols].astype(F32) + low).astype(BF16)
            y_copy(i).start()
            at(i, third)

        y_copy(n_chunks - 2).wait()
        y_copy(n_chunks - 1).wait()

    with jax.named_scope("mlp"):
        pl.run_scoped(
            mlp,
            pltpu.VMEM(w1_hbm.shape, BF16), pltpu.VMEM(w2_hbm.shape, BF16),
            pltpu.VMEM((2, chunk, dim), BF16), pltpu.VMEM((2, chunk, dim), BF16), pltpu.VMEM((chunk, hid), BF16),
            pltpu.SemaphoreType.DMA((2,)), pltpu.SemaphoreType.DMA((2,)), pltpu.SemaphoreType.DMA((2,)),
        )

    def head(z):
        w_load.wait()
        with jax.named_scope("xfinish"):
            x_finish()

        kept = mask_ref[...]
        count = jnp.maximum(jnp.sum(kept, keepdims=True), 1.0)
        wgt[...] = kept / count

        def row_iota(rows):
            return lax.broadcasted_iota(jnp.int32, (rows, tb), 0)

        def logits_phase(zraw):
            @pl.loop(0, ring)
            def _(b):
                xb = xg[pl.ds(pl.multiple_of(b * tb, tb), tb), :]
                lab = lab_ref[pl.ds(b, 1), :]
                tops, sums, tgt = [], [], jnp.zeros((1, tb), F32)
                def logits(q):
                    zt = lax.dot_general(wv[q * QT:(q + 1) * QT, :], xb, NT, preferred_element_type=F32)
                    if (q + 1) * QT > vocab:
                        zt = jnp.where(row_iota(QT) + q * QT < vocab, zt, NEG)
                    zraw[q % 2] = zt

                logits(0)
                for q in range(nq):
                    if q + 1 < nq:
                        logits(q + 1)
                    zt = zraw[q % 2]
                    top = jnp.max(zt, axis=0, keepdims=True)
                    e = jnp.exp(zt - top)
                    z[b, q * QT:(q + 1) * QT, :] = e
                    tgt = tgt + down(jnp.where(row_iota(QT) + q * QT == lab, zt, 0.0))
                    sums.append(down(e))
                    tops.append(top)
                    mst[q, pl.ds(b, 1), :] = top
                peak = functools.reduce(jnp.maximum, tops)
                total = sum(s * jnp.exp(t - peak) for s, t in zip(sums, tops))
                stat_tx[pl.ds(b, 1), :] = peak + jnp.log(total)
                tp_tx[pl.ds(b, 1), :] = tgt * mask_ref[pl.ds(b, 1), :]
                at(b, [(k, side[3 + k]) for k in range(8)])

        with jax.named_scope("logits"):
            pl.run_scoped(logits_phase, pltpu.VMEM((2, QT, tb), F32))

        def stat_copy(p):
            return remote(stat_tx, stat_rx.at[me], st_ss.at[p], st_rs.at[p], {"pp": lax.rem(me + p, n)})

        def tp_copy(p):
            return remote(tp_rx.at[pl.ds(n, 1)], tp_rx.at[pl.ds(me, 1)], tp_ss.at[p], tp_rs.at[p], {"pp": lax.rem(me + p, n)})

        with jax.named_scope("stats"):
            order = [n // 2] + [q for k in range(1, n // 2) for q in (n // 2 - k, n // 2 + k)]
            for p in order:
                stat_copy(p).start()
            stat_rx[me] = stat_tx[...]
            mine = jnp.sum(tp_tx[...], keepdims=True)
            tp_rx[pl.ds(n, 1), :] = jnp.broadcast_to(mine, (1, 128))
            tp_rx[pl.ds(me, 1), :] = jnp.broadcast_to(mine, (1, 128))
            for p in order:
                tp_copy(p).start()

            @pl.loop(0, vpad // 128)
            def _(t):
                o = pl.multiple_of(t * 128, 128)
                wt[:, pl.ds(o, 128)] = wv[pl.ds(o, 128), :].T

            for p in range(1, n):
                stat_copy(p).wait_recv()
            peak = stat_rx[0]
            for p in range(1, n):
                peak = jnp.maximum(peak, stat_rx[p])
            total = jnp.exp(stat_rx[0] - peak)
            for p in range(1, n):
                total = total + jnp.exp(stat_rx[p] - peak)
            lse = peak + jnp.log(total)
            for q in range(nq):
                scale[q] = jnp.exp(mst[q] - lse) * wgt[...]
            lse_sum = jnp.sum(kept * lse, keepdims=True)

        def r_both(k, far, first):
            for d in range(2):
                r_emit(d, k, far, first)

        def dest(t):
            k = jnp.where(t == 0, 4, 3 - (t - 1) // 2)
            k = jnp.where(t == 0, 4, k * (1 - 2 * lax.rem(jnp.maximum(t - 1, 0), 2)))
            return chip(k)

        def pw(t):
            r_share(dest(t), t).wait_recv()

        def first_4():
            pw(0)
            r_both(4, OUTER, FIRST)

        def first_3r():
            pw(1)
            r_emit(0, 3, INNER, FIRST)

        def first_3l():
            pw(2)
            r_emit(1, 3, INNER, FIRST)

        def acc_2():
            pw(3)
            pw(4)
            r_both(2, INNER, LATER)

        dx_events = [(1, first_4), (2, first_3r), (3, first_3l), (5, lambda: r_both(3, OUTER, LATER))]
        dx_side = [(0, side[11]), (1, side[12]), (3, side[13]), (5, lambda: h_final(h0_out))]

        def blocks(gbuf):
            @pl.loop(0, ring)
            def _(t):
                b = dest(t)
                lab = lab_ref[pl.ds(b, 1), :]
                wrow = wgt[pl.ds(b, 1), :]
                for q in range(nq):
                    g = z[b, q * QT:(q + 1) * QT, :] * scale[q, pl.ds(b, 1), :]
                    g = g - jnp.where(row_iota(QT) + q * QT == lab, wrow, 0.0)
                    gbuf[q * QT:(q + 1) * QT, :] = g.astype(BF16)
                res = jnp.dot(wt[...], gbuf[...], preferred_element_type=F32)
                dxo[b, 0] = res[:, :hb]
                dxo[b, 1] = res[:, hb:]
                r_share(b, t).start()
                at(t, dx_events)
                at(t, dx_side)

        with jax.named_scope("dxblocks"):
            pl.run_scoped(blocks, pltpu.VMEM((vpad, tb), BF16))

        def tables(ga, wbuf, wsem):
            def w_copy(i, rows):
                slot = lax.rem(i, 2)
                return pltpu.make_async_copy(wbuf.at[slot, pl.ds(0, rows)], dw_hbm.at[pl.ds(pl.multiple_of(i * WT, 8), rows)], wsem.at[slot])

            tail = vocab - (nw - 1) * WT

            def acc_1():
                pw(5)
                pw(6)
                r_both(1, INNER, LATER)

            dw_events = [(0, acc_2), (3, lambda: r_both(2, OUTER, LATER)), (6, acc_1), (9, lambda: r_both(1, OUTER, LATER))]

            def fill(i, gt):
                o = pl.multiple_of(i * WT, WT)
                q = i // (QT // WT)
                rid = row_iota(WT) + i * WT
                for b in range(ring):
                    g = z[b, pl.ds(o, WT), :] * scale[q, b:b + 1, :]
                    g = g - jnp.where(rid == lab_ref[b:b + 1, :], wgt[b:b + 1, :], 0.0)
                    gt[:, b * tb:(b + 1) * tb] = g.astype(BF16)

            @pl.loop(0, nw)
            def _(i):
                slot = lax.rem(i, 2)
                fill(i, ga)

                @pl.when(i >= 2)
                def _():
                    w_copy(i - 2, WT).wait()

                wbuf[slot] = jnp.dot(ga[...], xg[...], preferred_element_type=F32)

                @pl.when(i < nw - 1)
                def _():
                    w_copy(i, WT).start()

                at(i, dw_events)

            w_copy(nw - 1, tail).start()
            w_copy(nw - 2, WT).wait()
            w_copy(nw - 1, tail).wait()

        d_finish()
        with jax.named_scope("tables"):
            pl.run_scoped(
                tables,
                pltpu.VMEM((WT, ring * tb), BF16),
                pltpu.VMEM((2, WT, dim), F32), pltpu.SemaphoreType.DMA((2,)),
            )

        with jax.named_scope("tail"):
            pw(7)
            r_final(dx_out)
            for p in range(1, n):
                tp_copy(p).wait_recv()
            target = down(tp_rx[0:n, :])
            loss_out[...] = jnp.broadcast_to((lse_sum - target) / count, loss_out.shape)
            for p in range(1, n):
                stat_copy(p).wait_send()
                tp_copy(p).wait_send()
            for t in range(ring):
                r_share(dest(jnp.int32(t)), t).wait_send()

    pl.run_scoped(
        head,
        pltpu.VMEM((ring, vpad, tb), F32),
    )
    with jax.named_scope("drain"):
        x_drain()
        d_drain()
        r_drain()
        h_drain()
        for k in range(ring):
            h_share(lax.rem(j + k, ring), k).wait_send()

def compact(rank, base, cells):
    rows = lax.broadcasted_iota(jnp.int32, (PICK, rank.shape[1]), 0) + base
    for b in range(rank.shape[0]):
        width = rank.shape[1]
        cells[:, b * width:(b + 1) * width] = jnp.where(rows == rank[b:b + 1, :], 1.0, 0.0).astype(BF16)


def positions(cells, digits):
    two = lax.dot_general(digits[...], cells[...], NT, preferred_element_type=F32)
    return (two[0:1] * 64.0 + two[8:9]).astype(jnp.int32)


def pick_rows(vocab, emb_scale, ints, w_hbm, emb, lab, mask, rank, count, digits, wv, cells, hits, sem):
    ring, tb = lab.shape
    vpad = wv.shape[0]
    wv[vpad - 64:, :] = jnp.zeros((64, wv.shape[1]), BF16)
    load = pltpu.make_async_copy(w_hbm, wv.at[pl.ds(0, vocab)], sem)
    load.start()
    offset = lax.axis_index("pp") * vocab
    here = ints[0:ring, :] - offset
    lab[...] = jnp.where((here >= 0) & (here < vocab), here, -1)
    mask[...] = ints[ring:2 * ring, :].astype(F32)
    pos = ints[2 * ring:, :] - offset
    inside = (pos >= 0) & (pos < vocab)
    flag = jnp.where(inside, 1.0, 0.0)
    tri = jnp.where(
        lax.broadcasted_iota(jnp.int32, (tb, tb), 0) <= lax.broadcasted_iota(jnp.int32, (tb, tb), 1), 1.0, 0.0
    ).astype(BF16)
    upto = jnp.dot(flag.astype(BF16), tri, preferred_element_type=F32)
    row = lax.broadcasted_iota(jnp.int32, (ring, tb), 0)
    before = jnp.zeros((1, 1), F32)
    for b in range(ring):
        upto = upto + jnp.where(row == b, before, 0.0)
        before = before + jnp.sum(flag[b:b + 1, :], axis=1, keepdims=True)
    rank[...] = jnp.where(inside, upto.astype(jnp.int32) - 1, -1)
    count[...] = jnp.broadcast_to(before.astype(jnp.int32), count.shape)
    safe = jnp.where(inside, pos, 0)
    for b in range(ring):
        cols = slice(b * tb, (b + 1) * tb)
        digits[0:8, cols] = jnp.broadcast_to((safe[b:b + 1, :] // 64).astype(F32), (8, tb)).astype(BF16)
        digits[8:16, cols] = jnp.broadcast_to(lax.rem(safe[b:b + 1, :], 64).astype(F32), (8, tb)).astype(BF16)
    emb[...] = jnp.zeros(emb.shape, BF16)
    total = jnp.max(before).astype(jnp.int32)
    load.wait()

    @pl.loop(0, (total + PICK - 1) // PICK)
    def _(k):
        compact(rank[...], k * PICK, cells)
        where = positions(cells, digits)
        step = 640
        for v in range(0, vpad, step):
            rows = lax.broadcasted_iota(jnp.int32, (step, PICK), 0) + v
            hits[v:v + step, :] = jnp.where(rows == where, 1.0, 0.0).astype(BF16)
        rows = lax.dot_general(hits[...], wv[...], TN, preferred_element_type=F32)
        rows = (rows * emb_scale).astype(BF16)
        for t in range(0, emb.shape[0], 512):
            spread = lax.dot_general(cells[:, t:t + 512], rows, TN, preferred_element_type=F32)
            emb[t:t + 512, :] = emb[t:t + 512, :] + spread.astype(BF16)


def finish(emb_scale, count, rank, digits, dg, dxt, h0_in, loss_in, acc, y_in, dw, y, dx, h0, loss, cells, picked, where):
    i = pl.program_id(0)
    chunks = (count[0, 0] + PICK - 1) // PICK

    @pl.when(i == 0)
    def _():
        @pl.loop(0, jnp.maximum(chunks, 1))
        def _(k):
            compact(rank[...], k * PICK, cells)
            where[pl.ds(k, 1), :] = positions(cells, digits)
            rows = jnp.dot(cells[...], dg[...], preferred_element_type=F32).astype(BF16)
            picked[pl.ds(pl.multiple_of(k * PICK, PICK), PICK), :] = rows

        dx[...] = dxt[...].T
        h0[...] = h0_in[...]
        loss[...] = loss_in[...]

    y[...] = y_in[...]
    rows = lax.broadcasted_iota(jnp.int32, (acc.shape[0], PICK), 0) + i * acc.shape[0]

    def part(k):
        hits = jnp.where(rows == where[pl.ds(k, 1), :], 1.0, 0.0).astype(BF16)
        return jnp.dot(hits, picked[pl.ds(pl.multiple_of(k * PICK, PICK), PICK), :], preferred_element_type=F32)

    table = lax.fori_loop(1, chunks, lambda k, t: t + part(k), part(0))
    dw[...] = (acc[...] + table * emb_scale).astype(BF16)


def solution(mesh):
    n = mesh.shape["pp"]
    ring = n // 2

    def local_step(x_rows, w_slice, labels, tok_mask, next_ids, d_rows, act_in, w_up, w_down):
        vocab, dim = w_slice.shape
        hb = x_rows.shape[0]
        tb = 2 * hb
        tokens = ring * tb
        vpad = -(-vocab // QT) * QT
        emb_scale = math.sqrt(dim)
        vmem = pl.BlockSpec(memory_space=pltpu.VMEM)
        hbm = pl.BlockSpec(memory_space=pltpu.HBM)
        dma = lambda *s: pltpu.SemaphoreType.DMA(s)
        arr = jax.ShapeDtypeStruct
        ints = jnp.concatenate([labels, tok_mask, next_ids]).reshape(3 * ring, tb)
        emb, lab, mask, rank, count, digits = pl.pallas_call(
            functools.partial(pick_rows, vocab, emb_scale),
            out_shape=[
                arr((tokens, dim), BF16), arr((ring, tb), jnp.int32), arr((ring, tb), F32), arr((ring, tb), jnp.int32),
                arr((8, 128), jnp.int32), arr((16, tokens), BF16),
            ],
            in_specs=[vmem, hbm],
            out_specs=[vmem] * 6,
            scratch_shapes=[
                pltpu.VMEM((vpad, dim), BF16), pltpu.VMEM((PICK, tokens), BF16), pltpu.VMEM((vpad, PICK), BF16), pltpu.SemaphoreType.DMA,
            ],
        )(ints, w_slice)
        dx, acc, h0, y, loss, dg = pl.pallas_call(
            functools.partial(body, n, vocab),
            out_shape=[
                arr((dim, hb), F32), arr((vocab, dim), F32), arr((hb, dim), BF16), arr(act_in.shape[1:], BF16),
                arr((8, 128), F32), arr((tokens, dim), BF16),
            ],
            in_specs=[vmem, vmem, hbm, vmem, vmem, hbm, hbm, hbm, hbm],
            out_specs=[vmem, hbm, vmem, hbm, vmem, hbm],
            scratch_shapes=[
                pltpu.VMEM((vpad, dim), BF16), pltpu.VMEM((dim, vpad), BF16),
                pltpu.VMEM((ring * tb, dim), BF16),
                pltpu.VMEM((ring, 2, dim, hb), F32), pltpu.VMEM((ring, dim, hb), F32), pltpu.VMEM((2, 5, dim, hb), F32),
                pltpu.VMEM((ring, hb, dim), BF16), pltpu.VMEM((ring, hb, dim), BF16), pltpu.VMEM((2, 5, hb, dim), BF16),
                pltpu.VMEM((n, ring, tb), F32), pltpu.VMEM((n + 8, 128), F32),
                pltpu.VMEM((ring, tb), F32), pltpu.VMEM((ring, tb), F32),
                pltpu.VMEM((vpad // QT, ring, tb), F32), pltpu.VMEM((vpad // QT, ring, tb), F32), pltpu.VMEM((ring, tb), F32),
            ] + [dma(2, 4, 2)] * 8 + [dma(2, 5, 2), dma(2, 5, 2), dma(ring), dma(ring)] * 2 + [dma(n)] * 4 + [dma(2), dma(ring)],
            compiler_params=pltpu.CompilerParams(collective_id=0, has_side_effects=True, vmem_limit_bytes=67043328),
        )(x_rows, d_rows, w_slice, lab, mask, act_in[0], w_up[0], w_down[0], emb)
        steps = 8
        vt = -(-vocab // (16 * steps)) * 16
        whole = lambda *s: pl.BlockSpec(s, lambda i: (0, 0))
        tile = lambda rows, cols: pl.BlockSpec((rows, cols), lambda i: (i, 0))
        dw, y, dx, h0, loss = pl.pallas_call(
            functools.partial(finish, emb_scale),
            grid=(steps,),
            out_shape=[
                arr((vocab, dim), BF16), arr(y.shape, BF16), arr((hb, dim), F32), arr((hb, dim), BF16), arr((8, 128), F32),
            ],
            in_specs=[
                pl.BlockSpec(memory_space=pltpu.SMEM), whole(ring, tb), whole(16, tokens), whole(tokens, dim),
                whole(dim, hb), whole(hb, dim), whole(8, 128), tile(vt, dim), tile(y.shape[0] // steps, dim),
            ],
            out_specs=[tile(vt, dim), tile(y.shape[0] // steps, dim), whole(hb, dim), whole(hb, dim), whole(8, 128)],
            scratch_shapes=[
                pltpu.VMEM((PICK, tokens), BF16), pltpu.VMEM((-(-tokens // PICK) * PICK, dim), BF16),
                pltpu.VMEM((max(8, -(-tokens // PICK)), PICK), jnp.int32),
            ],
        )(count, rank, digits, dg, dx, h0, loss, acc, y)
        return loss[0, :1], dx, dw, h0, y[None]

    token_spec = P(("dp", "pp"))
    return jax.shard_map(
        local_step,
        mesh=mesh,
        in_specs=(token_spec, P("pp"), P("dp"), P("dp"), P("dp"), token_spec, token_spec, P("pp"), P("pp")),
        out_specs=(P("dp"), token_spec, token_spec, token_spec, token_spec),
        check_vma=False,
    )
```

time: 160 us -> 136 us (0.85)
  local copies, waits for them, and re-layouts: 23.8 us -> 3.28 us
  other arithmetic: 4.22 us -> 0.61 us
    gather x1 -> x0, local copies, waits for them, and re-layouts: 11.4 us -> none  [local_step(): picked = w_slice[jnp.clip(pos, 0, vocab - 1)]]
    unnamed x8 -> x0, local copies, waits for them, and re-layouts: 9.31 us -> none
    convert_element_type x2 -> x0, other arithmetic: 2.79 us -> none  [the longest x1 2.09 us: local_step(): jnp.where(in_share[:, None], picked.astype(F32) * emb_scale, 0.0)]
    concatenate x0 -> x3, local copies, waits for them, and re-layouts: none -> 2.1 us  [local_step(): ints = jnp.concatenate([labels, tok_mask, next_ids]).reshape(3 * ring, tb)]
    reshape x3 -> x0, local copies, waits for them, and re-layouts: 1.81 us -> none  [the longest x1 0.6 us: local_step(): mask = tok_mask.astype(F32).reshape(ring, tb)]
    pallas_call x1 -> x3, Pallas kernels: 131 us -> 131 us  [the longest x1 108 us: local_step(): pl.pallas_call(functools.partial(body, n, vocab), out_shape=[arr((dim, hb...]
where the time goes in v2:
time: 136 us
  Pallas kernels  131 us (96%)
  local copies, waits for them, and re-layouts  3.28 us (2%)
    pallas_call x1, Pallas kernels, local_step(): pl.pallas_call(functools.partial(body, n, vocab), out_shape=[arr((dim, hb...  108 us
    pallas_call x1, Pallas kernels, local_step(): pl.pallas_call(functools.partial(finish, emb_scale), grid=(steps,), out_s...  14.6 us
    pallas_call x1, Pallas kernels, local_step(): pl.pallas_call(functools.partial(pick_rows, vocab, emb_scale), out_shape=...  8.56 us

profile of v2, /device:TPU:21, one launch (start us, length us, event | category | flops | bytes accessed | tf_op | source)
XLA Modules:
  0.0 135.7 jit_solution(8625733116552058610)
XLA Ops:
  0.6 0.7 concatenate.10
  1.3 0.7 concatenate.11
  2.0 0.7 concatenate.12
  2.7 0.6 pad_add_fusion.ints
  3.3 8.6 %shard_map.128 = (bf16[2048,768]{1,0:T(8,128)(2,1)}, s32[8,256]{1,0:T(8,128)}, f32[8,256]{1,0:T(8,128)}, s32[8,256]{1,0:T(8,128)}, s32[8,128]{1,0:T(8,128)}, /*index=5*/bf16[16,2048]{1,0:T(8,128)(2,1)}) custom-call(s32[24,256]{1,0:T(8,128)} %pad_add_fusion.ints, bf16[3144,768]{1,0:T(8,128)(2,1)} %w_hbm.3), custom_call_target="tpu_custom_call" | custom-call | tf_op jit(solution)/shard_map/pallas_call | solution.py:599
  11.9 108.0 %shard_map.129 = (f32[768,128]{1,0:T(8,128)}, f32[3144,768]{1,0:T(8,128)}, bf16[128,768]{1,0:T(8,128)(2,1)}, bf16[2048,768]{1,0:T(8,128)(2,1)}, f32[8,128]{1,0:T(8,128)}, /*index=5*/bf16[2048,768]{1,0:T(8,128)(2,1)}) custom-call(bf16[128,768]{1,0:T(8,128)(2,1)} %x_in.1, bf16[128,768]{1,0:T(8,128)(2,1)} %d_in.1, bf16[3144,768]{1,0:T(8,128)(2,1)} %w_hbm.3, ...), custom_call_target="tpu_custom_call" | custom-call | tf_op jit(solution)/shard_map/pallas_call | solution.py:611
  119.9 14.6 %shard_map.130 = (bf16[3144,768]{1,0:T(8,128)(2,1)}, bf16[2048,768]{1,0:T(8,128)(2,1)}, f32[128,768]{1,0:T(8,128)}, bf16[128,768]{1,0:T(8,128)(2,1)}, f32[8,128]{1,0:T(8,128)}) custom-call(s32[8,128]{1,0:T(8,128)} %get-tuple-element.22.count, s32[8,256]{1,0:T(8,128)} %get-tuple-element.23.rank, bf16[16,2048]{1,0:T(8,128)(2,1)} %get-tuple-element.24.digits, ...), custom_call_target="tpu_custom_call" | custom-call | tf_op jit(solution)/shard_map/pallas_call | solution.py:634
  134.5 1.2 slice.3
